TPU v7x, 32 devices: a whole 2x2x4 slice. The times are simulated.
32 devices in a mesh: rows: 4 (over z), vocab: 8 (over y, x, core).
Axes of the slice: x: 2, y: 2, z: 4, core: 2. Of those that a mesh axis runs over, the one named last changes fastest.
Arguments:
- hidden: bfloat16 [512, 8192], P('rows', 'vocab'), may hold values from -30 to 30
- head: bfloat16 [8192, 152064], P(None, ('vocab', 'rows')), may hold values from -1 to 1
- states: int32 [512], replicated, may hold values from 0 to 2047
- class_of: int32 [152064], P('vocab'), may hold values from 0 to 255, as said below
- table: int32 [2048, 8], replicated, may hold values from -2147483648 to 2147483646, as said below
Outputs:
- log_probs: float32 [512, 152064], P('rows', 'vocab')
- entropy: float32 [512], P('rows')
Inputs may be any that keep to these rules, and one draw needn't show every extreme that they name: `class_of`: class 0 is the class of at least one token. `table`: bit 0 of word 0 is set in every state, so class 0 is allowed everywhere.
All inputs are finite; a program needn't handle non-finite values.
Results may differ from a plain program's by a relative error of at most 0.0003.
Values may be sent and summed in bfloat16 or wider, within the bound.
A program may use at most 192 MiB of HBM per device.

v0:
```python
import jax
import jax.numpy as jnp
from jax import lax
from jax.sharding import PartitionSpec as P

masked_floor = -1e30


def token_mask(states, table, class_of):
    words = jnp.take(table, states, axis=0)
    shifts = lax.broadcasted_iota(jnp.int32, (1, 1, 32), 2)
    bit_values = jnp.bitwise_and(jnp.right_shift(words[:, :, None], shifts), 1)
    allowed_class = bit_values.reshape(words.shape[0], words.shape[1] * 32).astype(jnp.bfloat16)
    onehot = (
        lax.broadcasted_iota(jnp.int32, (allowed_class.shape[1], class_of.shape[0]), 0)
        == class_of[None, :]
    ).astype(jnp.bfloat16)
    return jnp.dot(allowed_class, onehot, preferred_element_type=jnp.float32) > 0.5


def masked_peak(logits, allowed):
    return jnp.max(jnp.where(allowed, logits, masked_floor), axis=1)


def weighted_sums(logits, allowed, peak):
    weights = jnp.where(allowed, jnp.exp(logits - peak[:, None]), 0.0)
    return (jnp.sum(weights, axis=1), jnp.sum(weights * logits, axis=1))


def finish(logits, allowed, peak, total, weighted):
    norm_log = peak + jnp.log(total)
    log_probs = jnp.where(allowed, logits - norm_log[:, None], 0.0)
    return (log_probs, norm_log - weighted / total)


def vocab_stats(logits, allowed):
    own_peak = masked_peak(logits, allowed)
    own_total, own_weighted = weighted_sums(logits, allowed, own_peak)
    parts = lax.all_gather(jnp.stack([own_peak, own_total, own_weighted]), "vocab", axis=0)
    peak = jnp.max(parts[:, 0], axis=0)
    factor = jnp.exp(parts[:, 0] - peak[None, :])
    return (peak, jnp.sum(factor * parts[:, 1], axis=0), jnp.sum(factor * parts[:, 2], axis=0))


levels = 65000.0


def encode(logits):
    high = jnp.max(logits, axis=1)
    low = jnp.min(logits, axis=1)
    middle = 0.5 * (high + low)
    width = jnp.maximum(high - low, 1e-30)
    scaled = (logits - middle[:, None]) * (levels / width)[:, None]
    return (jnp.round(scaled).astype(jnp.int32).astype(jnp.int16), jnp.stack([middle, width / levels], axis=1))


def to_row_groups(logits):
    groups = lax.axis_size("rows")
    rows, columns = logits.shape
    own = rows // groups
    codes, scales = encode(logits)
    codes = lax.all_to_all(codes.reshape(groups, own, columns), "rows", 0, 0)
    scales = lax.all_to_all(scales.reshape(groups, own, 2), "rows", 0, 0)
    values = codes.astype(jnp.float32) * scales[:, :, 1:2] + scales[:, :, 0:1]
    return jnp.transpose(values, (1, 0, 2)).reshape(own, groups * columns)


def on_device(hidden, head, states, class_of, table):
    all_rows = lax.all_gather(hidden, "rows", axis=0, tiled=True)
    logits = jnp.dot(
        lax.all_gather(all_rows, "vocab", axis=1, tiled=True),
        head,
        preferred_element_type=jnp.float32,
    )
    group = lax.axis_index("rows")
    own_count = states.shape[0] // lax.axis_size("rows")
    own_logits = to_row_groups(logits)
    own_states = lax.dynamic_slice_in_dim(states, group * own_count, own_count, 0)
    allowed = token_mask(own_states, table, class_of)
    peak, total, weighted = vocab_stats(own_logits, allowed)
    log_probs, entropy = finish(own_logits, allowed, peak, total, weighted)
    return (log_probs, entropy)


def solution(mesh):
    in_specs = (P("rows", "vocab"), P(None, ("vocab", "rows")), P(), P("vocab"), P())
    out_specs = (P("rows", "vocab"), P("rows"))
    return jax.shard_map(
        on_device, mesh=mesh, in_specs=in_specs, out_specs=out_specs, check_vma=False
    )
```

profile of v0, /device:TPU:0, one launch (start us, length us, event | category | flops | bytes accessed | tf_op | source)
XLA Modules:
  0.0 309.3 jit_solution(13070469323877328229)
XLA Ops:
  7.2 0.0 all-gather.5.cloned.1.call-start
  7.2 0.7 all-gather.5.cloned.1.call-update
  7.9 0.0 all-gather.7.cloned.1.call-start
  7.9 32.3 %all-gather.5.cloned.1.call-done = bf16[512,1024]{1,0:T(8,128)(2,1)} async-done(((bf16[128,1024]{1,0:T(8,128)(2,1)}), bf16[512,1024]{1,0:T(8,128)(2,1)}) %all-gather.5.cloned.1.call-update) | async-done | bytes 1048592 | tf_op jit(solution)/shard_map/all_gather | solution.py:69
  40.3 0.0 all-gather.7.cloned.1.call-update
  40.3 55.5 %all-gather.7.cloned.1.call-done = bf16[512,8192]{1,0:T(8,128)(2,1)} async-done(((bf16[512,1024]{1,0:T(8,128)(2,1)}), bf16[512,8192]{1,0:T(8,128)(2,1)}) %all-gather.7.cloned.1.call-update) | async-done | bytes 8388624 | tf_op jit(solution)/shard_map/all_gather | solution.py:71
  95.9 49.4 %fusion.10 = (f32[512]{0:T(512)S(1)}, f32[512]{0:T(512)S(1)}, f32[512,4752]{0,1:T(8,128)}) fusion(bf16[512,8192]{1,0:T(8,128)(2,1)} %all-gather.7.cloned.1.call-done, bf16[8192,4752]{0,1:T(8,128)(2,1)} %param.6), kind=kOutput, calls=%fused_computation.36 | convolution fusion | flops 39867531264 | bytes 95981568 | tf_op jit(solution)/shard_map/dot_general | solution.py:70
  145.3 0.6 pad_maximum_fusion
  145.9 4.6 %all-to-all-start.1 = ((f32[4,128,2]{1,2,0:T(2,128)}), f32[4,128,2]{1,2,0:T(2,128)S(1)}, u32[]{:S(2)}, u32[]{:S(2)}) async-start(f32[4,128,2]{1,2,0:T(2,128)} %pad_maximum_fusion), calls=%async_computation.1 | async-start | bytes 8192 | tf_op jit(solution)/shard_map/all_to_all | solution.py:63
  150.5 0.0 copy-start.1
  150.5 7.2 %copy_bitcast_fusion = s16[4,128,4752]{1,2,0:T(8,128)(2,1)} fusion(f32[512,4752]{0,1:T(8,128)} %get-tuple-element.20, f32[512]{0:T(512)S(1)} %get-tuple-element.16, f32[512]{0:T(512)S(1)} %get-tuple-element.17), kind=kLoop, calls=%fused_computation.17 | loop fusion | flops 12165120 | bytes 14602240 | tf_op jit(solution)/shard_map/reshape | solution.py:62
  157.7 0.0 all-to-all-done.1
  157.7 5.2 %all-to-all-start = ((s16[4,128,4752]{1,2,0:T(8,128)(2,1)}), s16[4,128,4752]{1,2,0:T(8,128)(2,1)}, u32[]{:S(2)}, u32[]{:S(2)}) async-start(s16[4,128,4752]{1,2,0:T(8,128)(2,1)} %copy_bitcast_fusion), calls=%async_computation | async-start | bytes 9732096 | tf_op jit(solution)/shard_map/all_to_all | solution.py:62
  162.9 0.0 copy-start.2
  162.9 0.1 shift_right_arithmetic.23
  163.0 0.0 copy-done.1
  163.0 0.3 copy.16
  163.4 0.8 compare_and_fusion
  164.1 0.6 gather_fusion
  164.8 0.1 broadcast_select_fusion
  164.9 0.1 fusion.9
  165.1 105.9 %all-to-all-done = s16[4,128,4752]{1,2,0:T(8,128)(2,1)} async-done(((s16[4,128,4752]{1,2,0:T(8,128)(2,1)}), s16[4,128,4752]{1,2,0:T(8,128)(2,1)}, u32[]{:S(2)}, u32[]{:S(2)}) %all-to-all-start) | async-done | bytes 4866080 | tf_op jit(solution)/shard_map/all_to_all | solution.py:62
  270.9 4.3 %multiply_add_fusion = f32[4,128,4752]{1,2,0:T(8,128)S(1)} fusion(s16[4,128,4752]{1,2,0:T(8,128)(2,1)} %all-to-all-done, f32[4,128]{1,0:T(4,128)S(1)} %bitcast.57, f32[4,128]{1,0:T(4,128)S(1)} %bitcast.56), kind=kLoop, calls=%fused_computation.14 | loop fusion | flops 7299072 | bytes 14602240 | tf_op jit(solution)/shard_map/add | solution.py:64
  275.2 0.0 copy-done.2
  275.2 0.0 copy-start
  275.2 6.1 %fusion.1 = (f32[128]{0:T(128)S(1)}, pred[128,19008]{0,1:T(8,128)(4,1)S(1)}) fusion(f32[4,128,4752]{1,2,0:T(8,128)S(1)} %multiply_add_fusion, bf16[128,256]{0,1:T(8,128)(2,1)S(1)} %fusion.9, s32[19008]{0:T(1024)S(1)} %copy-done.2), kind=kOutput, calls=%fused_computation.8 | convolution fusion | flops 1257873280 | bytes 12307200 | tf_op jit(solution)/shard_map/dot_general | solution.py:18
  281.3 0.0 copy-done
  281.3 2.9 fusion.4
  284.2 8.9 %all-gather.1 = f32[8,3,128]{2,1,0:T(4,128)S(1)} all-gather(f32[1,3,128]{2,1,0:T(4,128)S(1)} %maximum_bitcast_fusion), channel_id=2, replica_groups=mesh['rows'=4,'vocab'=8] {'vocab'}, dimensions={0}, use_global_device_ids=true | all-gather | bytes 13824 | tf_op jit(solution)/shard_map/all_gather | solution.py:39
  293.1 0.5 divide_subtract_fusion
  293.6 8.8 %fusion.6 = f32[128,19008]{0,1:T(8,128)} fusion(pred[128,19008]{0,1:T(8,128)(4,1)S(1)} %get-tuple-element.22, f32[4,128,4752]{1,2,0:T(8,128)} %copy-done, f32[128]{0:T(128)S(1)} %get-tuple-element.19), kind=kLoop, calls=%fused_computation.13 | loop fusion | flops 4866048 | bytes 21897728 | tf_op jit(solution)/shard_map/jit(_where)/select_n | solution.py:32
  (9 shorter events, 0.1 us)
Async XLA Ops:
  7.2 33.1 %all-gather.5.cloned.1.call-start = ((), (), s32[]{:S(2)}) async-start(), calls=%async_computation.2 | async-start | bytes 1310720 | tf_op jit(solution)/shard_map/all_gather | solution.py:69
  7.9 88.0 %all-gather.7.cloned.1.call-start = ((), (), s32[]{:S(2)}) async-start(), calls=%async_computation.3 | async-start | bytes 9437184 | tf_op jit(solution)/shard_map/all_gather | solution.py:71
  145.9 11.8 %all-to-all-start.1 = ((f32[4,128,2]{1,2,0:T(2,128)}), f32[4,128,2]{1,2,0:T(2,128)S(1)}, u32[]{:S(2)}, u32[]{:S(2)}) async-start(f32[4,128,2]{1,2,0:T(2,128)} %pad_maximum_fusion), calls=%async_computation.1 | async-start | bytes 8192 | tf_op jit(solution)/shard_map/all_to_all | solution.py:63
  150.5 12.6 %copy-start.1 = (s32[2048,8]{0,1:T(8,128)S(1)}, s32[2048,8]{0,1:T(8,128)}, u32[]{:S(2)}) copy-start(s32[2048,8]{0,1:T(8,128)} %param.9) | copy-start | bytes 196612
  157.7 113.2 %all-to-all-start = ((s16[4,128,4752]{1,2,0:T(8,128)(2,1)}), s16[4,128,4752]{1,2,0:T(8,128)(2,1)}, u32[]{:S(2)}, u32[]{:S(2)}) async-start(s16[4,128,4752]{1,2,0:T(8,128)(2,1)} %copy_bitcast_fusion), calls=%async_computation | async-start | bytes 9732096 | tf_op jit(solution)/shard_map/all_to_all | solution.py:62
  162.9 112.3 %copy-start.2 = (s32[19008]{0:T(1024)S(1)}, s32[19008]{0:T(1024)}, u32[]{:S(2)}) copy-start(s32[19008]{0:T(1024)} %param.8) | copy-start | bytes 228100
  275.2 6.1 %copy-start = (f32[4,128,4752]{1,2,0:T(8,128)}, f32[4,128,4752]{1,2,0:T(8,128)S(1)}, u32[]{:S(2)}) copy-start(f32[4,128,4752]{1,2,0:T(8,128)S(1)} %multiply_add_fusion) | copy-start | bytes 29196292
Sparse Core Ops, SparseCore 0:
  9.5 30.6 all-gather.4
  42.2 53.6 all-gather.6
where the time goes:
time: 310 us; the launch traced here: 309 us
  waiting for transfers between devices  194 us (63%)
  matrix products  55.4 us (18%)
  other arithmetic  25.4 us (8%)
  between operations  14.2 us (5%)
  starting transfers between devices  9.88 us (3%)
  blocking collectives  8.87 us (3%)
    all_to_all x1, waiting for transfers between devices, to_row_groups(): codes = lax.all_to_all(codes.reshape(groups, own, columns), 'rows', 0, 0)  106 us
    all_gather x1, waiting for transfers between devices, on_device(): lax.all_gather(all_rows, 'vocab', axis=1, tiled=True)  55.5 us
    dot_general x1, matrix products, on_device(): jnp.dot(lax.all_gather(all_rows, 'vocab', axis=1, tiled=True), head, pref...  49.4 us
    all_gather x1, waiting for transfers between devices, on_device(): all_rows = lax.all_gather(hidden, 'rows', axis=0, tiled=True)  32.3 us
    all_gather x1, blocking collectives, vocab_stats(): lax.all_gather(jnp.stack([own_peak, own_total, own_weighted]), 'vocab', a...  8.87 us
    select_n x1, other arithmetic, finish(): log_probs = jnp.where(allowed, logits - norm_log[:, None], 0.0)  8.82 us
    reshape x1, other arithmetic, to_row_groups(): codes = lax.all_to_all(codes.reshape(groups, own, columns), 'rows', 0, 0)  7.23 us
  transfers between devices with their start and end apart: 4, of which 3 were waited for; matrix products, arithmetic and copies ran while one was open for 3% of the time, Pallas kernels for 0%

commit v1 on v0

v1 whole, which is shorter than its diff:
```python
import functools

import jax
import jax.numpy as jnp
from jax import lax
from jax.experimental import pallas as pl
from jax.experimental.pallas import tpu as pltpu
from jax.sharding import PartitionSpec as P

MESH = pl.DeviceIdType.MESH
LANES = 128
BIG = 1e30
LEVELS = 65000.0
SHIFT = 32500
FORBIDDEN = -32768
MAX_CHUNKS = 11
BUFFERS = 3
PIECES = 2
SUB = 144


def chunk_count(columns):
    for n in range(MAX_CHUNKS, 1, -1):
        if columns % n == 0 and (columns // n) % 16 == 0:
            return n
    return 1


def flip(v, bits):
    for bit in bits:
        size = 1 << bit
        v = v + size * (1 - 2 * lax.rem(lax.div(v, size), 2))
    return v


def subsets(bits):
    found = [()]
    for bit in bits:
        found = found + [s + (bit,) for s in found]
    return found


def exchange_kernel(
    nz, nv, hidden, head, states, class_of, table, codes_out, base_out, step_out, result,
    hid, buf, codes, banned, classes, onehot, x, scale_rows, scale_land, stat_own, stat_land,
    z_send, z_recv, f_send, h_send, h_recv, own_sem, head_sem, c_send, c_recv, s_send, s_recv, loc_sem, t_send, t_recv,
):
    rows, width = hidden.shape
    columns = head.shape[0]
    n = codes.shape[1]
    size = columns // n
    half = nz // 2
    piece = rows // PIECES
    steps = nv.bit_length() - 1
    z = lax.axis_index("rows")
    v = lax.axis_index("vocab")
    side = lax.div(z, half)
    far_base = (1 - side) * half
    near_base = side * half

    def send(src, dst, ssem, rsem, zz, vv):
        return pltpu.make_async_remote_copy(
            src_ref=src, dst_ref=dst, send_sem=ssem, recv_sem=rsem, device_id=(zz, vv), device_id_type=MESH
        )

    def z_peer(j):
        return lax.rem(z + j, nz)

    def v_peer(j):
        return lax.rem(v + j, nv)

    barrier = pltpu.get_barrier_semaphore()
    for j in range(1, nz):
        pl.semaphore_signal(barrier, inc=1, device_id=(z_peer(j), v), device_id_type=MESH)
    for j in range(1, nv):
        pl.semaphore_signal(barrier, inc=1, device_id=(z, v_peer(j)), device_id_type=MESH)

    def head_copy(t):
        at = lax.rem(t, BUFFERS)
        start = pl.multiple_of(lax.rem(t, n) * size, 16) if n > 1 else 0
        return pltpu.make_async_copy(head.at[pl.ds(start, size), :], buf.at[at], head_sem.at[at])

    for t in range(min(BUFFERS, 2 * n)):
        head_copy(jnp.int32(t)).start()

    pl.semaphore_wait(barrier, nz - 1 + nv - 1)

    def slot(zz, p, vv):
        return hid.at[zz, pl.ds(p * piece, piece), pl.ds(pl.multiple_of(vv * width, width), width)]

    def own(p):
        return hidden.at[pl.ds(p * piece, piece), :]

    def far(k):
        return (1 - side) * (half + k) + side * (half - 1 - k)

    def near(j):
        return near_base + lax.rem(z - near_base + j, half)

    inner = (1 - side) * half + side * (half - 1)
    outward = jnp.clip(z - 1 + 2 * side, 0, nz - 1)
    outermost = side * (nz - 1)

    def cross(p):
        return send(own(p), slot(z, p, v), z_send.at[0, p], z_recv.at[z, p], inner, v)

    def beside(j, p):
        return send(own(p), slot(z, p, v), z_send.at[j, p], z_recv.at[z, p], near(j), v)

    def onward(k, p):
        zz = far(k)
        return send(slot(zz, p, v), slot(zz, p, v), f_send.at[k, p], z_recv.at[zz, p], outward, v)

    def arrived(zz, p):
        send(slot(zz, p, v), slot(zz, p, v), z_send.at[0, p], z_recv.at[zz, p], z, v).wait_recv()

    for p in range(PIECES):
        cross(p).start()
    for j in range(1, half):
        for p in range(PIECES):
            beside(j, p).start()
    for p in range(PIECES):
        pltpu.make_async_copy(own(p), slot(z, p, v), own_sem.at[p]).start()

    def order(p):
        upper = list(range(1, steps))
        if p % 2:
            upper = upper[::-1]
        return upper + [0]

    def spread(q, zz, p, s, is_own):
        bits = order(p)
        partner = flip(v, [bits[s]])
        for m in subsets(bits[:s]):
            vv = flip(v, m)
            src = own(p) if (is_own and not m) else slot(zz, p, vv)
            send(src, slot(zz, p, vv), h_send.at[q, p, s], h_recv.at[q, p, s], z, partner).start()

    def spread_step(q, p, s):
        block = hid.at[0, pl.ds(p * piece, piece), pl.ds(0, width << s)]
        return send(block, block, h_send.at[q, p, s], h_recv.at[q, p, s], z, v)

    for zz in range(nz):
        @pl.when(z == zz)
        def _(zz=zz):
            classes[:, pl.ds(0, columns)] = class_of[:, zz * columns:(zz + 1) * columns]

    n_classes = onehot.shape[1]
    kinds = lax.broadcasted_iota(jnp.int32, (LANES, n_classes), 1)
    for b in range(-(-columns // LANES)):
        some = min(LANES, columns - b * LANES)
        line = classes[:, b * LANES:(b + 1) * LANES]
        turned = jnp.transpose(jnp.broadcast_to(line, (LANES, LANES)))
        wide = jnp.concatenate([turned] * (n_classes // LANES), axis=1)
        hot = jnp.where(wide == kinds, 1.0, 0.0).astype(jnp.bfloat16)
        onehot[b * LANES:b * LANES + some, :] = hot[:some]

    n_words, n_states = table.shape
    n_bytes = 4 * n_words
    packed = table[...]
    parts = [jnp.bitwise_and(jnp.right_shift(packed, 8 * b), 255) for b in range(4)]
    octets = jnp.concatenate(parts, axis=0).astype(jnp.float32).astype(jnp.bfloat16)
    which = lax.broadcasted_iota(jnp.int32, (n_states, rows), 0)
    bits8 = lax.broadcasted_iota(jnp.int32, (8, rows), 0)
    for g in range(nz):
        hot = jnp.where(which == states[:, g * rows:(g + 1) * rows], 1.0, 0.0).astype(jnp.bfloat16)
        found = jnp.dot(octets, hot, preferred_element_type=jnp.float32).astype(jnp.int32)
        blocks = []
        for w in range(n_words):
            for b in range(4):
                line = found[b * n_words + w:b * n_words + w + 1, :]
                bit = jnp.bitwise_and(jnp.right_shift(jnp.broadcast_to(line, (8, rows)), bits8), 1)
                blocks.append(jnp.where(bit > 0, 0.0, -BIG))
        banned[g] = jnp.concatenate(blocks, axis=0).astype(jnp.bfloat16)

    def running(g):
        return scale_rows.at[g, pl.ds(2 * n, 8), :]

    for g in range(nz):
        first = lax.broadcasted_iota(jnp.int32, (8, rows), 0) == 0
        scale_rows[g, 2 * n:2 * n + 8, :] = jnp.where(first, -BIG, 0.0)

    for k in range(half):
        for p in range(PIECES):
            arrived(far(k), p)

            @pl.when(z != outermost)
            def _(k=k, p=p):
                onward(k, p).start()

            spread(k, far(k), p, 0, False)
    for s in range(1, steps):
        for k in range(half):
            for p in range(PIECES):
                spread_step(k, p, s - 1).wait_recv()
                spread(k, far(k), p, s, False)

    def near_event(s):
        for j in range(half):
            for p in range(PIECES):
                if s > 0:
                    spread_step(half + j, p, s - 1).wait_recv()
                elif j == 0:
                    pltpu.make_async_copy(own(p), slot(z, p, v), own_sem.at[p]).wait()
                else:
                    arrived(near(j), p)
                if s < steps:
                    spread(half + j, near(j), p, s, j == 0)

    near_event(0)
    for k in range(half):
        for p in range(PIECES):
            spread_step(k, p, steps - 1).wait_recv()

    n_rows = half * rows

    def encode(g, i, lanes):
        values = x[:, lanes]
        high = jnp.max(values, axis=0, keepdims=True)
        low = jnp.min(jnp.where(values > -0.1 * BIG, values, BIG), axis=0, keepdims=True)
        gap = jnp.maximum(high - low, 1e-30)
        rate = LEVELS / gap
        total = jnp.zeros((1, rows), jnp.float32)
        weighted = jnp.zeros((1, rows), jnp.float32)
        for r in range(0, size, SUB):
            end = min(r + SUB, size)
            values = x[r:end, lanes]
            level = jnp.maximum((values - low) * rate + 0.5, float(FORBIDDEN + SHIFT))
            codes[g, i, r:end, :] = (level.astype(jnp.int32) - SHIFT).astype(jnp.int16)
            weights = jnp.exp(values - high)
            total = total + jnp.sum(weights, axis=0, keepdims=True)
            weighted = weighted + jnp.sum(weights * values, axis=0, keepdims=True)
        step = gap * (1.0 / LEVELS)
        scale_rows[g, pl.ds(i, 1), :] = low + SHIFT * step
        scale_rows[g, pl.ds(n + i, 1), :] = step
        old = scale_rows[g, 2 * n:2 * n + 3, :]
        peak = jnp.maximum(old[0:1], high)
        f0 = jnp.exp(old[0:1] - peak)
        f1 = jnp.exp(high - peak)
        scale_rows[g, 2 * n:2 * n + 1, :] = peak
        scale_rows[g, 2 * n + 1:2 * n + 2, :] = f0 * old[1:2] + f1 * total
        scale_rows[g, 2 * n + 2:2 * n + 3, :] = f0 * old[2:3] + f1 * weighted

    def code_copy(g, i):
        return send(codes.at[g, i], codes_out.at[z, i], c_send.at[g], c_recv.at[z], g, v)

    def scale_copy(g):
        return send(scale_rows.at[g], scale_land.at[z], s_send.at[g], s_recv.at[z], g, v)

    def run_pass(index, base, events):
        def chunk_step(i, carry):
            t = index * n + i
            for e, event in enumerate(events):
                @pl.when(i == min(2 * e + 1, n - 1))
                def _(event=event):
                    event()
            head_copy(t).wait()
            weights = hid[pl.ds(base, half)].reshape(n_rows, hid.shape[2])
            got = lax.dot_general(
                buf[lax.rem(t, BUFFERS)], weights, (((1,), (1,)), ((), ())), preferred_element_type=jnp.float32
            )
            mine = onehot[pl.ds(pl.multiple_of(i * size, 16) if n > 1 else 0, size), :]
            for j in range(half):
                x[:, j * rows:(j + 1) * rows] = got[:, j * rows:(j + 1) * rows] + jnp.dot(
                    mine, banned[base + j], preferred_element_type=jnp.float32
                )

            @pl.when(t + BUFFERS < 2 * n)
            def _():
                head_copy(t + BUFFERS).start()

            for j in range(half):
                encode(base + j, i, slice(j * rows, (j + 1) * rows))
            for j in range(half):
                g = base + j
                if index == 0:
                    code_copy(g, i).start()
                else:
                    @pl.when(g != z)
                    def _(g=g):
                        code_copy(g, i).start()

                    @pl.when(g == z)
                    def _(g=g):
                        pltpu.make_async_copy(codes.at[g, i], codes_out.at[z, i], loc_sem).start()
            return carry

        lax.fori_loop(0, n, chunk_step, 0)
        for j in range(half):
            g = base + j
            if index == 0:
                scale_copy(g).start()
            else:
                @pl.when(g != z)
                def _(g=g):
                    scale_copy(g).start()

    run_pass(0, far_base, [functools.partial(near_event, s) for s in range(1, steps + 1)])
    run_pass(1, near_base, [])
    scale_land[z] = scale_rows[z]

    for j in range(1, nz):
        g = z_peer(j)
        send(scale_rows.at[g], scale_land.at[g], s_send.at[g], s_recv.at[g], z, v).wait_recv()

    def combine(ref, count, line):
        peaks, totals, weights = [
            jnp.concatenate([ref[q, line + k:line + k + 1, :] for q in range(count)], axis=0) for k in range(3)
        ]
        peak = jnp.max(peaks, axis=0, keepdims=True)
        factor = jnp.exp(peaks - peak)
        return (
            peak,
            jnp.sum(factor * totals, axis=0, keepdims=True),
            jnp.sum(factor * weights, axis=0, keepdims=True),
        )

    def stat_copy(j):
        return send(stat_own, stat_land.at[v], t_send.at[j], t_recv.at[v], z, v_peer(j))

    summed = jnp.concatenate([*combine(scale_land, nz, 2 * n), jnp.zeros((5, rows), jnp.float32)], axis=0)
    stat_own[...] = summed
    stat_land[v] = summed
    for j in range(1, nv):
        stat_copy(j).start()
    for j in range(1, nv):
        u = v_peer(j)
        send(stat_own, stat_land.at[u], t_send.at[j], t_recv.at[u], z, v).wait_recv()
    peak, total, weighted = combine(stat_land, nv, 0)
    norm = peak + jnp.log(total)
    result[...] = norm - weighted / total
    for g in range(nz):
        base_out[g] = scale_land[g, 0:n, :] - norm
        step_out[g] = scale_land[g, n:2 * n, :]

    for j in range(1, nz):
        g = z_peer(j)
        whole = send(codes.at[g], codes_out.at[g], c_send.at[g], c_recv.at[g], z, v)
        whole.wait_send()
        whole.wait_recv()
        scale_copy(g).wait_send()
    pltpu.make_async_copy(codes.at[z], codes_out.at[z], loc_sem).wait()
    for j in range(1, nv):
        stat_copy(j).wait_send()
    for p in range(PIECES):
        cross(p).wait_send()
        for j in range(1, half):
            beside(j, p).wait_send()

        @pl.when(z != outermost)
        def _(p=p):
            for k in range(half):
                onward(k, p).wait_send()

        for q in range(nz):
            for s in range(steps):
                spread_step(q, p, s).wait_send()


def exchange(nz, nv, hidden, head, states, class_of, table):
    rows, width = hidden.shape
    columns, depth = head.shape
    n = chunk_count(columns)
    size = columns // n
    lines = -(-(2 * n + 8) // 8) * 8
    steps = nv.bit_length() - 1
    half = nz // 2
    padded = -(-columns // LANES) * LANES
    n_classes = table.shape[0] * 32
    vmem = pl.BlockSpec(memory_space=pltpu.VMEM)
    hbm = pl.BlockSpec(memory_space=pl.ANY)
    dma = pltpu.SemaphoreType.DMA
    return pl.pallas_call(
        functools.partial(exchange_kernel, nz, nv),
        out_shape=[
            jax.ShapeDtypeStruct((nz, n, size, rows), jnp.int16),
            jax.ShapeDtypeStruct((nz, n, rows), jnp.float32),
            jax.ShapeDtypeStruct((nz, n, rows), jnp.float32),
            jax.ShapeDtypeStruct((1, rows), jnp.float32),
        ],
        in_specs=[vmem, hbm, vmem, vmem, vmem],
        out_specs=[hbm, vmem, vmem, vmem],
        scratch_shapes=[
            pltpu.VMEM((nz, rows, depth), jnp.bfloat16),
            pltpu.VMEM((BUFFERS, size, depth), jnp.bfloat16),
            pltpu.VMEM((nz, n, size, rows), jnp.int16),
            pltpu.VMEM((nz, n_classes, rows), jnp.bfloat16),
            pltpu.VMEM((1, padded), jnp.int32),
            pltpu.VMEM((columns, n_classes), jnp.bfloat16),
            pltpu.VMEM((size, half * rows), jnp.float32),
            pltpu.VMEM((nz, lines, rows), jnp.float32),
            pltpu.VMEM((nz, lines, rows), jnp.float32),
            pltpu.VMEM((8, rows), jnp.float32),
            pltpu.VMEM((nv, 8, rows), jnp.float32),
            dma((half, PIECES)),
            dma((nz, PIECES)),
            dma((half, PIECES)),
            dma((nz, PIECES, steps)),
            dma((nz, PIECES, steps)),
            dma((PIECES,)),
            dma((BUFFERS,)),
            dma((nz,)),
            dma((nz,)),
            dma((nz,)),
            dma((nz,)),
            dma,
            dma((nv,)),
            dma((nv,)),
        ],
        compiler_params=pltpu.CompilerParams(
            collective_id=0, has_side_effects=True, vmem_limit_bytes=62 * 1024 * 1024
        ),
    )(hidden, head, states, class_of, table)


def solution(mesh):
    nz, nv = mesh.shape["rows"], mesh.shape["vocab"]

    def on_device(hidden, head, states, class_of, table):
        codes, base, step, entropy = exchange(
            nz, nv, hidden, head.T, states.reshape(1, -1), class_of.reshape(1, -1), table.T
        )
        values = codes.astype(jnp.float32) * step[:, :, None, :] + base[:, :, None, :]
        log_probs = jnp.where(codes == FORBIDDEN, 0.0, values)
        return log_probs.reshape(-1, hidden.shape[0]).T, entropy.reshape(-1)

    in_specs = (P("rows", "vocab"), P(None, ("vocab", "rows")), P(), P("vocab"), P())
    out_specs = (P("rows", "vocab"), P("rows"))
    return jax.shard_map(on_device, mesh=mesh, in_specs=in_specs, out_specs=out_specs, check_vma=False)
```

time: 310 us -> 167 us (0.54)
  waiting for transfers between devices: 194 us -> 0 us
  Pallas kernels: 0 us -> 153 us
  matrix products: 55.4 us -> 0 us
  other arithmetic: 25.4 us -> 10.8 us
  between operations: 14.2 us -> 0.65 us
  starting transfers between devices: 9.88 us -> 0 us
  blocking collectives: 8.87 us -> 0 us
    pallas_call x0 -> x1, Pallas kernels: none -> 153 us  [exchange(): pl.pallas_call(functools.partial(exchange_kernel, nz, nv), out_shape=[jax...]
    all_to_all x2 -> x0, waiting for transfers between devices: 106 us -> none  [the longest x1 106 us: to_row_groups(): codes = lax.all_to_all(codes.reshape(groups, own, columns), 'rows', 0, 0)]
    all_gather x2 -> x0, waiting for transfers between devices: 87.9 us -> none  [the longest x1 55.5 us: on_device(): lax.all_gather(all_rows, 'vocab', axis=1, tiled=True)]
    dot_general x2 -> x0, matrix products: 55.4 us -> none  [the longest x1 49.4 us: on_device(): jnp.dot(lax.all_gather(all_rows, 'vocab', axis=1, tiled=True), head, pref...]
    all_to_all x2 -> x0, starting transfers between devices: 9.81 us -> none  [the longest x1 5.2 us: to_row_groups(): codes = lax.all_to_all(codes.reshape(groups, own, columns), 'rows', 0, 0)]
    all_gather x1 -> x0, blocking collectives: 8.87 us -> none  [vocab_stats(): lax.all_gather(jnp.stack([own_peak, own_total, own_weighted]), 'vocab', a...]
    reshape x1 -> x0, other arithmetic: 7.23 us -> none  [to_row_groups(): codes = lax.all_to_all(codes.reshape(groups, own, columns), 'rows', 0, 0)]
    add x1 -> x0, other arithmetic: 4.27 us -> none  [to_row_groups(): values = codes.astype(jnp.float32) * scales[:, :, 1:2] + scales[:, :, 0:1]]
  transfers between devices with their start and end apart: 4 -> 0, of which waited for: 3 -> 0; matrix products, arithmetic and copies ran while one was open for 3% -> 0% of each run, Pallas kernels for 0% -> 0%
where the time goes in v1:
time: 167 us
  Pallas kernels  153 us (92%)
  other arithmetic  10.8 us (6%)
  local copies, waits for them, and re-layouts  2.09 us (1%)
    pallas_call x1, Pallas kernels, exchange(): pl.pallas_call(functools.partial(exchange_kernel, nz, nv), out_shape=[jax...  153 us
    select_n x1, other arithmetic, on_device(): log_probs = jnp.where(codes == FORBIDDEN, 0.0, values)  10.8 us

profile of v1, /device:TPU:0, one launch (start us, length us, event | category | flops | bytes accessed | tf_op | source)
XLA Modules:
  0.0 166.8 jit_solution(8235581284167360318)
XLA Ops:
  0.6 1.6 reshape.19.class_of
  2.2 153.2 %shard_map.68 = (s16[4,11,432,128]{3,2,1,0:T(8,128)(2,1)}, f32[4,11,128]{2,1,0:T(8,128)}, f32[4,11,128]{2,1,0:T(8,128)}, f32[1,128]{1,0:T(1,128)}) custom-call(bf16[128,1024]{1,0:T(8,128)(2,1)} %hidden.1, bf16[4752,8192]{1,0:T(8,128)(2,1)} %bitcast.head, s32[1,512]{1,0:T(1,128)} %bitcast.9, s32[1,19008]{1,0:T(1,128)} %reshape.19.class_of, s32[8,2048]{1,0:T(8,128)} %bitcast.8), custom_call_target="tpu_custom_call" | custom-call | tf_op jit(solution)/shard_map/pallas_call | solution.py:373
  155.4 0.0 copy-start
  155.4 10.8 %add_select_fusion = f32[4,11,432,128]{3,2,1,0:T(8,128)} fusion(s16[4,11,432,128]{3,2,1,0:T(8,128)(2,1)} %get-tuple-element.6, f32[4,11,128]{2,1,0:T(8,128)} %get-tuple-element.8, f32[4,11,128]{2,1,0:T(8,128)} %get-tuple-element.7), kind=kLoop, calls=%fused_computation | loop fusion | flops 12165120 | bytes 14643200 | tf_op jit(solution)/shard_map/jit(_where)/select_n | solution.py:424
  166.3 0.0 copy-done
  166.3 0.5 copy.8
Async XLA Ops:
  155.4 10.8 %copy-start = (f32[1,128]{1,0:T(1,128)S(1)}, f32[1,128]{1,0:T(1,128)}, u32[]{:S(2)}) copy-start(f32[1,128]{1,0:T(1,128)} %get-tuple-element.9) | copy-start | bytes 1540

commit v2 on v1

--- a/solution.py
+++ b/solution.py
@@ -15,8 +15,11 @@
 FORBIDDEN = -32768
 MAX_CHUNKS = 11
 BUFFERS = 3
-PIECES = 2
+FEW_BUFFERS = 2
+PIECES = 4
 SUB = 144
+EXCHANGE_VMEM = 50 * 1024 * 1024
+DECODE_VMEM = 24 * 1024 * 1024
 
 
 def chunk_count(columns):
@@ -41,13 +44,15 @@
 
 
 def exchange_kernel(
-    nz, nv, hidden, head, states, class_of, table, codes_out, base_out, step_out, result,
-    hid, buf, codes, banned, classes, onehot, x, scale_rows, scale_land, stat_own, stat_land,
+    nz, nv, hidden, head, states_in, class_of, table_in, codes_out, base_out, step_out, result,
+    hid, buf, codes, banned, states, table, all_classes, classes, onehot, x, scale_rows, scale_land, stat_own, stat_land,
     z_send, z_recv, f_send, h_send, h_recv, own_sem, head_sem, c_send, c_recv, s_send, s_recv, loc_sem, t_send, t_recv,
+    class_sem,
 ):
     rows, width = hidden.shape
     columns = head.shape[0]
     n = codes.shape[1]
+    buffers = buf.shape[0]
     size = columns // n
     half = nz // 2
     piece = rows // PIECES
@@ -55,6 +60,7 @@
     z = lax.axis_index("rows")
     v = lax.axis_index("vocab")
     side = lax.div(z, half)
+    passes = 2
     far_base = (1 - side) * half
     near_base = side * half
 
@@ -76,11 +82,18 @@
         pl.semaphore_signal(barrier, inc=1, device_id=(z, v_peer(j)), device_id_type=MESH)
 
     def head_copy(t):
-        at = lax.rem(t, BUFFERS)
+        at = lax.rem(t, buffers)
         start = pl.multiple_of(lax.rem(t, n) * size, 16) if n > 1 else 0
         return pltpu.make_async_copy(head.at[pl.ds(start, size), :], buf.at[at], head_sem.at[at])
 
-    for t in range(min(BUFFERS, 2 * n)):
+    small = [
+        pltpu.make_async_copy(class_of, all_classes.at[0], class_sem.at[0]),
+        pltpu.make_async_copy(states_in, states, class_sem.at[1]),
+        pltpu.make_async_copy(table_in, table, class_sem.at[2]),
+    ]
+    for copy in small:
+        copy.start()
+    for t in range(min(buffers, passes * n)):
         head_copy(jnp.int32(t)).start()
 
     pl.semaphore_wait(barrier, nz - 1 + nv - 1)
@@ -94,31 +107,28 @@
     def far(k):
         return (1 - side) * (half + k) + side * (half - 1 - k)
 
-    def near(j):
-        return near_base + lax.rem(z - near_base + j, half)
-
-    inner = (1 - side) * half + side * (half - 1)
+    depth = (1 - side) * (half - 1 - z) + side * (z - half)
+    inward = z + 1 - 2 * side
     outward = jnp.clip(z - 1 + 2 * side, 0, nz - 1)
-    outermost = side * (nz - 1)
-
-    def cross(p):
-        return send(own(p), slot(z, p, v), z_send.at[0, p], z_recv.at[z, p], inner, v)
-
-    def beside(j, p):
-        return send(own(p), slot(z, p, v), z_send.at[j, p], z_recv.at[z, p], near(j), v)
-
-    def onward(k, p):
-        zz = far(k)
-        return send(slot(zz, p, v), slot(zz, p, v), f_send.at[k, p], z_recv.at[zz, p], outward, v)
+    has_outward = depth < half - 1
+
+    def near(e):
+        return (1 - side) * (half - 1 - e) + side * (half + e)
+
+    def own_inward(p):
+        return send(own(p), slot(z, p, v), z_send.at[0, p], z_recv.at[z, p], inward, v)
+
+    def own_outward(p):
+        return send(own(p), slot(z, p, v), z_send.at[1, p], z_recv.at[z, p], outward, v)
+
+    def onward(zz, p, target):
+        return send(slot(zz, p, v), slot(zz, p, v), f_send.at[zz, p], z_recv.at[zz, p], target, v)
 
     def arrived(zz, p):
-        send(slot(zz, p, v), slot(zz, p, v), z_send.at[0, p], z_recv.at[zz, p], z, v).wait_recv()
+        onward(zz, p, z).wait_recv()
 
     for p in range(PIECES):
-        cross(p).start()
-    for j in range(1, half):
-        for p in range(PIECES):
-            beside(j, p).start()
+        own_inward(p).start()
     for p in range(PIECES):
         pltpu.make_async_copy(own(p), slot(z, p, v), own_sem.at[p]).start()
 
@@ -128,22 +138,25 @@
             upper = upper[::-1]
         return upper + [0]
 
-    def spread(q, zz, p, s, is_own):
+    def spread(q, zz, p, s):
         bits = order(p)
         partner = flip(v, [bits[s]])
         for m in subsets(bits[:s]):
             vv = flip(v, m)
-            src = own(p) if (is_own and not m) else slot(zz, p, vv)
-            send(src, slot(zz, p, vv), h_send.at[q, p, s], h_recv.at[q, p, s], z, partner).start()
+            block = slot(zz, p, vv)
+            send(block, block, h_send.at[q, p, s], h_recv.at[q, p, s], z, partner).start()
 
     def spread_step(q, p, s):
         block = hid.at[0, pl.ds(p * piece, piece), pl.ds(0, width << s)]
         return send(block, block, h_send.at[q, p, s], h_recv.at[q, p, s], z, v)
 
+    for copy in small:
+        copy.wait()
+
     for zz in range(nz):
         @pl.when(z == zz)
         def _(zz=zz):
-            classes[:, pl.ds(0, columns)] = class_of[:, zz * columns:(zz + 1) * columns]
+            classes[:, pl.ds(0, columns)] = all_classes[:, zz * columns:(zz + 1) * columns]
 
     n_classes = onehot.shape[1]
     kinds = lax.broadcasted_iota(jnp.int32, (LANES, n_classes), 1)
@@ -180,39 +193,69 @@
         first = lax.broadcasted_iota(jnp.int32, (8, rows), 0) == 0
         scale_rows[g, 2 * n:2 * n + 8, :] = jnp.where(first, -BIG, 0.0)
 
-    for k in range(half):
+    def far_arrive(k):
         for p in range(PIECES):
             arrived(far(k), p)
 
-            @pl.when(z != outermost)
-            def _(k=k, p=p):
-                onward(k, p).start()
-
-            spread(k, far(k), p, 0, False)
+            @pl.when(has_outward)
+            def _(p=p):
+                onward(far(k), p, outward).start()
+
+            spread(k, far(k), p, 0)
+
+    def far_spread(k, s):
+        for p in range(PIECES):
+            spread_step(k, p, s - 1).wait_recv()
+            if s < steps:
+                spread(k, far(k), p, s)
+
+    def from_outside():
+        for e in range(1, half):
+            @pl.when(e > depth)
+            def _(e=e):
+                for p in range(PIECES):
+                    arrived(near(e), p)
+                    onward(near(e), p, inward).start()
+
+    def near_arrive():
+        for e in range(half - 1):
+            @pl.when(e < depth)
+            def _(e=e):
+                for p in range(PIECES):
+                    arrived(near(e), p)
+
+                    @pl.when(has_outward)
+                    def _(p=p):
+                        onward(near(e), p, outward).start()
+
+        for p in range(PIECES):
+            pltpu.make_async_copy(own(p), slot(z, p, v), own_sem.at[p]).wait()
+
+    def near_spread(s):
+        for e in range(half):
+            for p in range(PIECES):
+                if s > 0:
+                    spread_step(half + e, p, s - 1).wait_recv()
+                if s < steps:
+                    spread(half + e, near(e), p, s)
+
+    far_arrive(0)
+    from_outside()
+    for k in range(1, half):
+        far_arrive(k)
+
+    @pl.when(has_outward)
+    def _():
+        for p in range(PIECES):
+            own_outward(p).start()
+
     for s in range(1, steps):
         for k in range(half):
-            for p in range(PIECES):
-                spread_step(k, p, s - 1).wait_recv()
-                spread(k, far(k), p, s, False)
-
-    def near_event(s):
-        for j in range(half):
-            for p in range(PIECES):
-                if s > 0:
-                    spread_step(half + j, p, s - 1).wait_recv()
-                elif j == 0:
-                    pltpu.make_async_copy(own(p), slot(z, p, v), own_sem.at[p]).wait()
-                else:
-                    arrived(near(j), p)
-                if s < steps:
-                    spread(half + j, near(j), p, s, j == 0)
-
-    near_event(0)
+            far_spread(k, s)
+    near_arrive()
+    near_spread(0)
     for k in range(half):
-        for p in range(PIECES):
-            spread_step(k, p, steps - 1).wait_recv()
-
-    n_rows = half * rows
+        far_spread(k, steps)
 
     def encode(g, i, lanes):
         values = x[:, lanes]
@@ -247,56 +290,61 @@
     def scale_copy(g):
         return send(scale_rows.at[g], scale_land.at[z], s_send.at[g], s_recv.at[z], g, v)
 
-    def run_pass(index, base, events):
+    def run_pass(index, parts, events):
         def chunk_step(i, carry):
             t = index * n + i
-            for e, event in enumerate(events):
-                @pl.when(i == min(2 * e + 1, n - 1))
+            for at, event in events:
+                @pl.when(i == min(at, n - 1))
                 def _(event=event):
                     event()
             head_copy(t).wait()
-            weights = hid[pl.ds(base, half)].reshape(n_rows, hid.shape[2])
-            got = lax.dot_general(
-                buf[lax.rem(t, BUFFERS)], weights, (((1,), (1,)), ((), ())), preferred_element_type=jnp.float32
-            )
             mine = onehot[pl.ds(pl.multiple_of(i * size, 16) if n > 1 else 0, size), :]
-            for j in range(half):
-                x[:, j * rows:(j + 1) * rows] = got[:, j * rows:(j + 1) * rows] + jnp.dot(
-                    mine, banned[base + j], preferred_element_type=jnp.float32
+            for base, count, with_own in parts:
+                weights = hid[pl.ds(base, count)].reshape(count * rows, hid.shape[2])
+                got = lax.dot_general(
+                    buf[lax.rem(t, buffers)], weights, (((1,), (1,)), ((), ())), preferred_element_type=jnp.float32
                 )
-
-            @pl.when(t + BUFFERS < 2 * n)
+                for j in range(count):
+                    x[:, j * rows:(j + 1) * rows] = got[:, j * rows:(j + 1) * rows] + jnp.dot(
+                        mine, banned[base + j], preferred_element_type=jnp.float32
+                    )
+                for j in range(count):
+                    encode(base + j, i, slice(j * rows, (j + 1) * rows))
+                for j in range(count):
+                    g = base + j
+                    if not with_own:
+                        code_copy(g, i).start()
+                    else:
+                        @pl.when(g != z)
+                        def _(g=g):
+                            code_copy(g, i).start()
+
+                        @pl.when(g == z)
+                        def _(g=g):
+                            pltpu.make_async_copy(codes.at[g, i], codes_out.at[z, i], loc_sem).start()
+
+            @pl.when(t + buffers < passes * n)
             def _():
-                head_copy(t + BUFFERS).start()
-
-            for j in range(half):
-                encode(base + j, i, slice(j * rows, (j + 1) * rows))
-            for j in range(half):
+                head_copy(t + buffers).start()
+
+            return carry
+
+        lax.fori_loop(0, n, chunk_step, 0)
+        for base, count, with_own in parts:
+            for j in range(count):
                 g = base + j
-                if index == 0:
-                    code_copy(g, i).start()
+                if not with_own:
+                    scale_copy(g).start()
                 else:
                     @pl.when(g != z)
                     def _(g=g):
-                        code_copy(g, i).start()
-
-                    @pl.when(g == z)
-                    def _(g=g):
-                        pltpu.make_async_copy(codes.at[g, i], codes_out.at[z, i], loc_sem).start()
-            return carry
-
-        lax.fori_loop(0, n, chunk_step, 0)
-        for j in range(half):
-            g = base + j
-            if index == 0:
-                scale_copy(g).start()
-            else:
-                @pl.when(g != z)
-                def _(g=g):
-                    scale_copy(g).start()
-
-    run_pass(0, far_base, [functools.partial(near_event, s) for s in range(1, steps + 1)])
-    run_pass(1, near_base, [])
+                        scale_copy(g).start()
+
+    events = []
+    for s in range(1, steps + 1):
+        events.append(functools.partial(near_spread, s))
+    run_pass(0, [(far_base, half, False)], list(zip([1, 5, 8] + [n - 1] * steps, events)))
+    run_pass(1, [(near_base, half, True)], [])
     scale_land[z] = scale_rows[z]
 
     for j in range(1, nz):
@@ -343,14 +391,22 @@
     for j in range(1, nv):
         stat_copy(j).wait_send()
     for p in range(PIECES):
-        cross(p).wait_send()
-        for j in range(1, half):
-            beside(j, p).wait_send()
-
-        @pl.when(z != outermost)
+        own_inward(p).wait_send()
+
+        @pl.when(has_outward)
         def _(p=p):
+            own_outward(p).wait_send()
             for k in range(half):
-                onward(k, p).wait_send()
+                onward(far(k), p, outward).wait_send()
+
+        for e in range(half):
+            @pl.when(e > depth)
+            def _(e=e, p=p):
+                onward(near(e), p, inward).wait_send()
+
+            @pl.when(jnp.logical_and(e < depth, has_outward))
+            def _(e=e, p=p):
+                onward(near(e), p, outward).wait_send()
 
         for q in range(nz):
             for s in range(steps):
@@ -363,6 +419,7 @@
     n = chunk_count(columns)
     size = columns // n
     lines = -(-(2 * n + 8) // 8) * 8
+    buffers = BUFFERS if n > 1 else FEW_BUFFERS
     steps = nv.bit_length() - 1
     half = nz // 2
     padded = -(-columns // LANES) * LANES
@@ -373,18 +430,21 @@
     return pl.pallas_call(
         functools.partial(exchange_kernel, nz, nv),
         out_shape=[
-            jax.ShapeDtypeStruct((nz, n, size, rows), jnp.int16),
-            jax.ShapeDtypeStruct((nz, n, rows), jnp.float32),
-            jax.ShapeDtypeStruct((nz, n, rows), jnp.float32),
-            jax.ShapeDtypeStruct((1, rows), jnp.float32),
+            pltpu.VMEM((nz, n, size, rows), jnp.int16),
+            pltpu.VMEM((nz, n, rows), jnp.float32),
+            pltpu.VMEM((nz, n, rows), jnp.float32),
+            pltpu.VMEM((1, rows), jnp.float32),
         ],
-        in_specs=[vmem, hbm, vmem, vmem, vmem],
+        in_specs=[pl.BlockSpec(memory_space=pltpu.HBM)] * 5,
         out_specs=[hbm, vmem, vmem, vmem],
         scratch_shapes=[
             pltpu.VMEM((nz, rows, depth), jnp.bfloat16),
-            pltpu.VMEM((BUFFERS, size, depth), jnp.bfloat16),
+            pltpu.VMEM((buffers, size, depth), jnp.bfloat16),
             pltpu.VMEM((nz, n, size, rows), jnp.int16),
             pltpu.VMEM((nz, n_classes, rows), jnp.bfloat16),
+            pltpu.VMEM(states.shape, jnp.int32),
+            pltpu.VMEM(table.shape, jnp.int32),
+            pltpu.VMEM((1, class_of.shape[0]), jnp.int32),
             pltpu.VMEM((1, padded), jnp.int32),
             pltpu.VMEM((columns, n_classes), jnp.bfloat16),
             pltpu.VMEM((size, half * rows), jnp.float32),
@@ -392,13 +452,13 @@
             pltpu.VMEM((nz, lines, rows), jnp.float32),
             pltpu.VMEM((8, rows), jnp.float32),
             pltpu.VMEM((nv, 8, rows), jnp.float32),
-            dma((half, PIECES)),
+            dma((2, PIECES)),
             dma((nz, PIECES)),
-            dma((half, PIECES)),
+            dma((nz, PIECES)),
             dma((nz, PIECES, steps)),
             dma((nz, PIECES, steps)),
             dma((PIECES,)),
-            dma((BUFFERS,)),
+            dma((buffers,)),
             dma((nz,)),
             dma((nz,)),
             dma((nz,)),
@@ -406,22 +466,46 @@
             dma,
             dma((nv,)),
             dma((nv,)),
+            dma((3,)),
         ],
         compiler_params=pltpu.CompilerParams(
-            collective_id=0, has_side_effects=True, vmem_limit_bytes=62 * 1024 * 1024
+            collective_id=0, has_side_effects=True, vmem_limit_bytes=EXCHANGE_VMEM
         ),
     )(hidden, head, states, class_of, table)
 
 
+def decode_kernel(codes, base, step, entropy, log_probs, entropy_out):
+    i = pl.program_id(0)
+    entropy_out[...] = entropy[...]
+    for g in range(codes.shape[0]):
+        level = codes[g, i].astype(jnp.int32)
+        value = level.astype(jnp.float32) * step[g, pl.ds(i, 1), :] + base[g, pl.ds(i, 1), :]
+        log_probs[g, 0] = jnp.where(level == FORBIDDEN, 0.0, value)
+
+
+def decode(codes, base, step, entropy):
+    nz, n, size, rows = codes.shape
+    line = pl.BlockSpec((1, rows), lambda i: (0, 0))
+    block = pl.BlockSpec((nz, 1, size, rows), lambda i: (0, i, 0, 0))
+    return pl.pallas_call(
+        decode_kernel,
+        grid=(n,),
+        in_specs=[pl.BlockSpec(memory_space=pltpu.VMEM)] * 4,
+        out_specs=[block, line],
+        out_shape=[
+            jax.ShapeDtypeStruct(codes.shape, jnp.float32),
+            jax.ShapeDtypeStruct((1, rows), jnp.float32),
+        ],
+        compiler_params=pltpu.CompilerParams(dimension_semantics=("arbitrary",), vmem_limit_bytes=DECODE_VMEM),
+    )(codes, base, step, entropy)
+
+
 def solution(mesh):
     nz, nv = mesh.shape["rows"], mesh.shape["vocab"]
 
     def on_device(hidden, head, states, class_of, table):
-        codes, base, step, entropy = exchange(
-            nz, nv, hidden, head.T, states.reshape(1, -1), class_of.reshape(1, -1), table.T
-        )
-        values = codes.astype(jnp.float32) * step[:, :, None, :] + base[:, :, None, :]
-        log_probs = jnp.where(codes == FORBIDDEN, 0.0, values)
+        coded = exchange(nz, nv, hidden, head.T, states.reshape(1, -1), class_of, table.T)
+        log_probs, entropy = decode(*coded)
         return log_probs.reshape(-1, hidden.shape[0]).T, entropy.reshape(-1)
 
     in_specs = (P("rows", "vocab"), P(None, ("vocab", "rows")), P(), P("vocab"), P())

time: 167 us -> 158 us (0.946)
  other arithmetic: 10.8 us -> 0 us
  Pallas kernels: 153 us -> 157 us
  local copies, waits for them, and re-layouts: 2.09 us -> 0 us
    select_n x1 -> x0, other arithmetic: 10.8 us -> none  [on_device(): log_probs = jnp.where(codes == FORBIDDEN, 0.0, values)]
    pallas_call x1 -> x2, Pallas kernels: 153 us -> 157 us  [the longest x1 150 us: exchange(): pl.pallas_call(functools.partial(exchange_kernel, nz, nv), out_shape=[plt...]
where the time goes in v2:
time: 158 us
  Pallas kernels  157 us (99%)
    pallas_call x1, Pallas kernels, exchange(): pl.pallas_call(functools.partial(exchange_kernel, nz, nv), out_shape=[plt...  150 us
    pallas_call x1, Pallas kernels, decode(): pl.pallas_call(decode_kernel, grid=(n,), in_specs=[pl.BlockSpec(memory_sp...  6.54 us

profile of v2, /device:TPU:0, one launch (start us, length us, event | category | flops | bytes accessed | tf_op | source)
XLA Modules:
  0.0 157.5 jit_solution(7981647685002290006)
XLA Ops:
  0.6 150.3 %shard_map.68 = (s16[4,11,432,128]{3,2,1,0:T(8,128)(2,1)S(1)}, f32[4,11,128]{2,1,0:T(8,128)S(1)}, f32[4,11,128]{2,1,0:T(8,128)S(1)}, f32[1,128]{1,0:T(1,128)S(1)}) custom-call(bf16[128,1024]{1,0:T(8,128)(2,1)} %hidden.1, bf16[4752,8192]{1,0:T(8,128)(2,1)} %bitcast.head, s32[1,512]{1,0:T(1,128)} %bitcast.8, s32[19008]{0:T(1024)} %class_of.1, s32[8,2048]{1,0:T(8,128)} %bitcast.7), custom_call_target="tpu_custom_call" | custom-call | tf_op jit(solution)/shard_map/pallas_call | solution.py:430
  151.0 6.5 %shard_map.69 = (f32[4,11,432,128]{3,2,1,0:T(8,128)}, f32[1,128]{1,0:T(1,128)}) custom-call(s16[4,11,432,128]{3,2,1,0:T(8,128)(2,1)S(1)} %get-tuple-element.8.codes, f32[4,11,128]{2,1,0:T(8,128)S(1)} %get-tuple-element.9.base, f32[4,11,128]{2,1,0:T(8,128)S(1)} %get-tuple-element.10.step, f32[1,128]{1,0:T(1,128)S(1)} %get-tuple-element.11.entropy), custom_call_target="tpu_custom_call" | custom-call | tf_op jit(solution)/shard_map/pallas_call | solution.py:490

commit v3 on v2

--- a/solution.py
+++ b/solution.py
@@ -13,11 +13,12 @@
 LEVELS = 65000.0
 SHIFT = 32500
 FORBIDDEN = -32768
-MAX_CHUNKS = 11
+MAX_CHUNKS = 9
 BUFFERS = 3
 FEW_BUFFERS = 2
 PIECES = 4
-SUB = 144
+SUB = 176
+PACE = 3
 EXCHANGE_VMEM = 50 * 1024 * 1024
 DECODE_VMEM = 24 * 1024 * 1024
 
@@ -241,19 +242,20 @@
 
     far_arrive(0)
     from_outside()
-    for k in range(1, half):
-        far_arrive(k)
+    for k in range(half):
+        if k > 0:
+            far_arrive(k)
+        if steps > 1:
+            far_spread(k, 1)
 
     @pl.when(has_outward)
     def _():
         for p in range(PIECES):
             own_outward(p).start()
 
-    for s in range(1, steps):
+    for s in range(2, steps):
         for k in range(half):
             far_spread(k, s)
-    near_arrive()
-    near_spread(0)
     for k in range(half):
         far_spread(k, steps)
 
@@ -290,6 +292,10 @@
     def scale_copy(g):
         return send(scale_rows.at[g], scale_land.at[z], s_send.at[g], s_recv.at[z], g, v)
 
+    def send_far(k):
+        for j in range(half):
+            code_copy(far_base + j, k).start()
+
     def run_pass(index, parts, events):
         def chunk_step(i, carry):
             t = index * n + i
@@ -312,9 +318,7 @@
                     encode(base + j, i, slice(j * rows, (j + 1) * rows))
                 for j in range(count):
                     g = base + j
-                    if not with_own:
-                        code_copy(g, i).start()
-                    else:
+                    if with_own:
                         @pl.when(g != z)
                         def _(g=g):
                             code_copy(g, i).start()
@@ -326,6 +330,14 @@
             @pl.when(t + buffers < passes * n)
             def _():
                 head_copy(t + buffers).start()
+
+            late = lax.div(t - 1, PACE) + 1
+            k = jnp.where(t < 2, t, late)
+            due = jnp.logical_or(t < 2, jnp.logical_and(t > PACE, lax.rem(t - 1, PACE) == 0))
+
+            @pl.when(jnp.logical_and(due, k < n))
+            def _():
+                send_far(k)
 
             return carry
 
@@ -340,11 +352,21 @@
                     def _(g=g):
                         scale_copy(g).start()
 
-    events = []
+    def near_start():
+        near_arrive()
+        near_spread(0)
+
+    events = [near_start]
     for s in range(1, steps + 1):
         events.append(functools.partial(near_spread, s))
-    run_pass(0, [(far_base, half, False)], list(zip([1, 5, 8] + [n - 1] * steps, events)))
+    run_pass(0, [(far_base, half, False)], list(zip([0, 2, 5, 7] + [n - 1] * steps, events)))
     run_pass(1, [(near_base, half, True)], [])
+
+    def send_rest(k, carry):
+        send_far(k)
+        return carry
+
+    lax.fori_loop(min(n, 2 + (2 * n - 2) // PACE), n, send_rest, 0)
     scale_land[z] = scale_rows[z]
 
     for j in range(1, nz):

time: 158 us -> 147 us (0.930)
  Pallas kernels: 157 us -> 145 us
    pallas_call x1, Pallas kernels: 150 us -> 139 us  [exchange(): pl.pallas_call(functools.partial(exchange_kernel, nz, nv), out_shape=[plt...]
where the time goes in v3:
time: 147 us; the launch traced here: 146 us
  Pallas kernels  145 us (99%)
    pallas_call x1, Pallas kernels, exchange(): pl.pallas_call(functools.partial(exchange_kernel, nz, nv), out_shape=[plt...  139 us
    pallas_call x1, Pallas kernels, decode(): pl.pallas_call(decode_kernel, grid=(n,), in_specs=[pl.BlockSpec(memory_sp...  5.99 us

profile of v3, /device:TPU:0, one launch (start us, length us, event | category | flops | bytes accessed | tf_op | source)
XLA Modules:
  0.0 145.7 jit_solution(13810057988729956322)
XLA Ops:
  0.6 139.1 %shard_map.68 = (s16[4,9,528,128]{3,2,1,0:T(8,128)(2,1)S(1)}, f32[4,9,128]{2,1,0:T(8,128)S(1)}, f32[4,9,128]{2,1,0:T(8,128)S(1)}, f32[1,128]{1,0:T(1,128)S(1)}) custom-call(bf16[128,1024]{1,0:T(8,128)(2,1)} %hidden.1, bf16[4752,8192]{1,0:T(8,128)(2,1)} %bitcast.head, s32[1,512]{1,0:T(1,128)} %bitcast.8, s32[19008]{0:T(1024)} %class_of.1, s32[8,2048]{1,0:T(8,128)} %bitcast.7), custom_call_target="tpu_custom_call" | custom-call | tf_op jit(solution)/shard_map/pallas_call | solution.py:452
  139.7 6.0 %shard_map.69 = (f32[4,9,528,128]{3,2,1,0:T(8,128)}, f32[1,128]{1,0:T(1,128)}) custom-call(s16[4,9,528,128]{3,2,1,0:T(8,128)(2,1)S(1)} %get-tuple-element.8.codes, f32[4,9,128]{2,1,0:T(8,128)S(1)} %get-tuple-element.9.base, f32[4,9,128]{2,1,0:T(8,128)S(1)} %get-tuple-element.10.step, f32[1,128]{1,0:T(1,128)S(1)} %get-tuple-element.11.entropy), custom_call_target="tpu_custom_call" | custom-call | tf_op jit(solution)/shard_map/pallas_call | solution.py:512

commit v4 on v3

--- a/solution.py
+++ b/solution.py
@@ -19,6 +19,7 @@
 PIECES = 4
 SUB = 176
 PACE = 3
+EARLY = 1
 EXCHANGE_VMEM = 50 * 1024 * 1024
 DECODE_VMEM = 24 * 1024 * 1024
 
@@ -62,6 +63,7 @@
     v = lax.axis_index("vocab")
     side = lax.div(z, half)
     passes = 2
+    early = min(EARLY, n) if half > 1 else 0
     far_base = (1 - side) * half
     near_base = side * half
 
@@ -252,12 +254,6 @@
     def _():
         for p in range(PIECES):
             own_outward(p).start()
-
-    for s in range(2, steps):
-        for k in range(half):
-            far_spread(k, s)
-    for k in range(half):
-        far_spread(k, steps)
 
     def encode(g, i, lanes):
         values = x[:, lanes]
@@ -296,6 +292,22 @@
         for j in range(half):
             code_copy(far_base + j, k).start()
 
+    def send_far_rest(k):
+        for j in range(1, half):
+            code_copy(far(j), k).start()
+
+    def multiply(i, at, base, count):
+        start = i * size if isinstance(i, int) else pl.multiple_of(i * size, 16)
+        mine = onehot[pl.ds(start if n > 1 else 0, size), :]
+        weights = hid[pl.ds(base, count)].reshape(count * rows, hid.shape[2])
+        got = lax.dot_general(buf[at], weights, (((1,), (1,)), ((), ())), preferred_element_type=jnp.float32)
+        for j in range(count):
+            x[:, j * rows:(j + 1) * rows] = got[:, j * rows:(j + 1) * rows] + jnp.dot(
+                mine, banned[base + j], preferred_element_type=jnp.float32
+            )
+        for j in range(count):
+            encode(base + j, i, slice(j * rows, (j + 1) * rows))
+
     def run_pass(index, parts, events):
         def chunk_step(i, carry):
             t = index * n + i
@@ -303,19 +315,25 @@
                 @pl.when(i == min(at, n - 1))
                 def _(event=event):
                     event()
-            head_copy(t).wait()
-            mine = onehot[pl.ds(pl.multiple_of(i * size, 16) if n > 1 else 0, size), :]
+            if index == 0 and early:
+                @pl.when(i >= early)
+                def _():
+                    head_copy(t).wait()
+            else:
+                head_copy(t).wait()
+            at = lax.rem(t, buffers)
             for base, count, with_own in parts:
-                weights = hid[pl.ds(base, count)].reshape(count * rows, hid.shape[2])
-                got = lax.dot_general(
-                    buf[lax.rem(t, buffers)], weights, (((1,), (1,)), ((), ())), preferred_element_type=jnp.float32
-                )
-                for j in range(count):
-                    x[:, j * rows:(j + 1) * rows] = got[:, j * rows:(j + 1) * rows] + jnp.dot(
-                        mine, banned[base + j], preferred_element_type=jnp.float32
-                    )
-                for j in range(count):
-                    encode(base + j, i, slice(j * rows, (j + 1) * rows))
+                if with_own or not early:
+                    multiply(i, at, base, count)
+                else:
+                    @pl.when(i < early)
+                    def _():
+                        multiply(i, at, (1 - side) * (half + 1), half - 1)
+
+                    if early < n:
+                        @pl.when(i >= early)
+                        def _(base=base, count=count):
+                            multiply(i, at, base, count)
                 for j in range(count):
                     g = base + j
                     if with_own:
@@ -335,7 +353,13 @@
             k = jnp.where(t < 2, t, late)
             due = jnp.logical_or(t < 2, jnp.logical_and(t > PACE, lax.rem(t - 1, PACE) == 0))
 
-            @pl.when(jnp.logical_and(due, k < n))
+            due = jnp.logical_and(due, k < n)
+
+            @pl.when(jnp.logical_and(due, k < early))
+            def _():
+                send_far_rest(k)
+
+            @pl.when(jnp.logical_and(due, k >= early))
             def _():
                 send_far(k)
 
@@ -351,6 +375,16 @@
                     @pl.when(g != z)
                     def _(g=g):
                         scale_copy(g).start()
+
+    for s in range(2, steps + 1):
+        far_spread(0, s)
+    for i in range(early):
+        head_copy(jnp.int32(i)).wait()
+        multiply(i, i, far(0), 1)
+        code_copy(far(0), i).start()
+    for s in range(2, steps + 1):
+        for k in range(1, half):
+            far_spread(k, s)
 
     def near_start():
         near_arrive()

time: 147 us -> 146 us (level)
  no operation moved by 1% of the time
where the time goes in v4:
time: 146 us; the launch traced here: 145 us
  Pallas kernels  145 us (99%)
    pallas_call x1, Pallas kernels, exchange(): pl.pallas_call(functools.partial(exchange_kernel, nz, nv), out_shape=[plt...  139 us
    pallas_call x1, Pallas kernels, decode(): pl.pallas_call(decode_kernel, grid=(n,), in_specs=[pl.BlockSpec(memory_sp...  5.99 us

profile of v4, /device:TPU:0, one launch (start us, length us, event | category | flops | bytes accessed | tf_op | source)
XLA Modules:
  0.0 145.4 jit_solution(10329641385820191924)
XLA Ops:
  0.6 138.8 %shard_map.68 = (s16[4,9,528,128]{3,2,1,0:T(8,128)(2,1)S(1)}, f32[4,9,128]{2,1,0:T(8,128)S(1)}, f32[4,9,128]{2,1,0:T(8,128)S(1)}, f32[1,128]{1,0:T(1,128)S(1)}) custom-call(bf16[128,1024]{1,0:T(8,128)(2,1)} %hidden.1, bf16[4752,8192]{1,0:T(8,128)(2,1)} %bitcast.head, s32[1,512]{1,0:T(1,128)} %bitcast.8, s32[19008]{0:T(1024)} %class_of.1, s32[8,2048]{1,0:T(8,128)} %bitcast.7), custom_call_target="tpu_custom_call" | custom-call | tf_op jit(solution)/shard_map/pallas_call | solution.py:486
  139.4 6.0 %shard_map.69 = (f32[4,9,528,128]{3,2,1,0:T(8,128)}, f32[1,128]{1,0:T(1,128)}) custom-call(s16[4,9,528,128]{3,2,1,0:T(8,128)(2,1)S(1)} %get-tuple-element.8.codes, f32[4,9,128]{2,1,0:T(8,128)S(1)} %get-tuple-element.9.base, f32[4,9,128]{2,1,0:T(8,128)S(1)} %get-tuple-element.10.step, f32[1,128]{1,0:T(1,128)S(1)} %get-tuple-element.11.entropy), custom_call_target="tpu_custom_call" | custom-call | tf_op jit(solution)/shard_map/pallas_call | solution.py:546
